TPU v7x, 32 devices: a whole 2x2x4 slice. The times are simulated.
32 devices in a mesh: gx: 4 (over z), yz: 8 (over y, x, core).
Axes of the slice: x: 2, y: 2, z: 4, core: 2. Of those that a mesh axis runs over, the one named last changes fastest.
Arguments:
- brick_ids: int32 [4096, 1], P(('gx', 'yz')), may hold values from 0 to 31; in each aligned block of 128 rows (0 to 127, 128 to 255, ...) at most 4 rows name the same one
- voxel_offset: int32 [4096, 256], P(('gx', 'yz')), may hold values from 0 to 4095
- fractions: float32 [4096, 3, 256], P(('gx', 'yz')), may hold values from 0 to 1
- normals: float32 [4096, 3, 256], P(('gx', 'yz')), may hold values from -6 to 6
- point_weight: float32 [4096, 256], P(('gx', 'yz')), may hold values from 0.1 to 10
- tile_count: int32 [32], P(('gx', 'yz')), may hold values from 96 to 128, as said below
Outputs:
- rhs: float32 [16, 64, 128], P('gx', 'yz')
- screen: float32 [16, 64, 128], P('gx', 'yz')
Inputs may be any that keep to these rules, and one draw needn't show every extreme that they name: `brick_ids`: brick b belongs to index b // 8 of gx and b % 8 of yz. Among the 128 tile slots of one device no brick is named more than 4 times. `tile_count`: some device has all its slots valid in every draw.
All inputs are finite; a program needn't handle non-finite values.
Results may differ from a plain program's by a relative error of at most 0.0039.
Values sent between devices are 32-bit elements; how exact they have to be, the bound alone decides.
A program may use at most 64 MiB of HBM per device.

v0:
```python
import functools

import jax
import jax.numpy as jnp
from jax import lax
from jax.experimental import pallas as pl
from jax.experimental.pallas import tpu as pltpu
from jax.sharding import PartitionSpec as P

BX = 4
BY = 8
BZ = 128
MESH = pl.DeviceIdType.MESH
HALO_X = BX + 2
ROWS_Y = 2 * BY
X_CH = 4 * HALO_X
CHANNELS = X_CH + 19
PACK = 16


def spline(frac):
    weights = [0.5 * (1.0 - frac) ** 2, 0.75 - (frac - 0.5) ** 2, 0.5 * frac * frac]
    slopes = [frac - 1.0, 1.0 - 2.0 * frac, frac]
    return (weights, slopes)


def pick(masks, values):
    out = jnp.zeros_like(values[0])
    for mask, value in zip(masks, values):
        out = jnp.where(mask, value, out)
    return out


def prepare(rows, off_ref, frac_ref, norm_ref, weight_ref, chan):
    parts, lanes = chan.shape[1], chan.shape[3]

    def keep(n, value):
        for part in range(parts):
            chan[n, part, rows, :] = value[:, part * lanes : (part + 1) * lanes]

    offset = off_ref[rows, :]
    z_bits, y_bits = BZ.bit_length() - 1, BY.bit_length() - 1
    cell_x = offset >> (z_bits + y_bits)
    cell_y = (offset >> z_bits) & (BY - 1)
    cell_z = offset & (BZ - 1)
    wx, gx = spline(frac_ref[0, rows, :])
    nx, ny, nz = norm_ref[0, rows, :], norm_ref[1, rows, :], norm_ref[2, rows, :]
    weight = weight_ref[rows, :]
    at = [cell_x == m for m in range(BX)]
    sources = ([nx * v for v in gx], [ny * v for v in wx], [nz * v for v in wx], [weight * v for v in wx])
    for i in range(HALO_X):
        for n, values in enumerate(sources):
            shifts = [k for k in range(3) if 0 <= i - k < BX]
            keep(4 * i + n, pick([at[i - k] for k in shifts], [values[k] for k in shifts]))
    wy, gy = spline(frac_ref[1, rows, :])
    wz, gz = spline(frac_ref[2, rows, :])
    near = [cell_z + (k - 1) for k in range(3)]
    shift = PACK.bit_length() - 1
    rest = [cell_y.astype(jnp.float32)] + wy + gy + wz + gz
    rest += [(z & (PACK - 1)).astype(jnp.float32) for z in near] + [(z >> shift).astype(jnp.float32) for z in near]
    for n, value in enumerate(rest):
        keep(X_CH + n, value)


def stage_orders(n_columns):
    bits = n_columns.bit_length() - 1
    rest = list(range(1, bits))
    first = [0] if bits else []
    return [first + rest, first + rest[::-1]]


def fused_kernel(
    capacity, n_slabs, n_columns, table_ref, off_ref, frac_ref, norm_ref, weight_ref, out_ref,
    chan, left_a, left_b, third_a, third_b, val_a, val_b, der_a, der_b, grid, done, z_main, z_low, z_high,
    send_sem, recv_sem, send_z, recv_z, *stages
):
    tiles, tile_len = off_ref.shape
    orders = stage_orders(n_columns)
    steps = len(orders[0])
    starts = stages[:2]
    got = (stages[2 : 2 + steps], stages[2 + steps : 2 + 2 * steps])
    sums = (stages[2 + 2 * steps : 1 + 3 * steps], stages[1 + 3 * steps : 4 * steps])
    me_x, me_y = lax.axis_index("gx"), lax.axis_index("yz")
    bufs = ((left_a, third_a, val_a, der_a), (left_b, third_b, val_b, der_b))

    def slab_of(step):
        return lax.rem(me_x + 1 + step, n_slabs)

    def bit_of(k):
        return lax.rem(me_y // (1 << k), 2)

    def partner(k):
        return (me_x, me_y + (1 - 2 * bit_of(k)) * (1 << k))

    barrier = pltpu.get_barrier_semaphore()
    for k in range(steps):
        pl.semaphore_signal(barrier, inc=1, device_id=partner(k), device_id_type=MESH)
    for hop in range(1, n_slabs):
        other = (lax.rem(me_x + hop, n_slabs), me_y)
        pl.semaphore_signal(barrier, inc=1, device_id=other, device_id_type=MESH)

    def prepare_rows(step, _):
        prepare(pl.ds(pl.multiple_of(step * 8, 8), 8), off_ref, frac_ref, norm_ref, weight_ref, chan)
        return 0

    lax.fori_loop(0, tiles // 8, prepare_rows, 0)
    grid[...] = jnp.zeros_like(grid)

    lanes = tile_len
    row_y = lax.broadcasted_iota(jnp.int32, (ROWS_Y, lanes), 0)
    row_y = jnp.where(row_y == ROWS_Y - 1, -1, row_y).astype(jnp.float32)
    row_z = lax.broadcasted_iota(jnp.int32, (PACK, lanes), 0).astype(jnp.float32)
    edge = lax.broadcasted_iota(jnp.int32, (HALO_X, BY, BZ), 1)
    last = n_slabs * n_columns - 1

    def build(g, buf):
        left, third, val, der = buf
        brick = slab_of(g // n_columns) * n_columns + lax.rem(g, n_columns)
        for c in range(capacity):
            entry = table_ref[brick * capacity + c]
            away = jnp.where(entry >= 0, 0.0, 1.0) * (4.0 * BY)
            tile = jnp.maximum(entry, 0)
            for part in range(tile_len // lanes):
                cols = pl.ds(c * tile_len + part * lanes, lanes)

                def row(n):
                    return chan[n, part, pl.ds(tile, 1), :]

                gap = row_y - (row(X_CH) + away)
                hit = [gap == k - 1.0 for k in range(3)]
                wy = pick(hit, [jnp.broadcast_to(row(X_CH + 1 + k), gap.shape) for k in range(3)])
                gy = pick(hit, [jnp.broadcast_to(row(X_CH + 4 + k), gap.shape) for k in range(3)])
                for i in range(HALO_X):
                    band = pl.ds(i * ROWS_Y, ROWS_Y)
                    low = pl.ds((HALO_X + i) * ROWS_Y, ROWS_Y)
                    left[band, cols] = (row(4 * i) * wy + row(4 * i + 1) * gy).astype(jnp.bfloat16)
                    third[band, cols] = (row(4 * i + 2) * wy).astype(jnp.bfloat16)
                    left[low, cols] = (row(4 * i + 3) * wy).astype(jnp.bfloat16)
                hit = [row_z == row(X_CH + 13 + k) for k in range(3)]

                def spread(n, other):
                    for k in range(3):
                        other = jnp.where(hit[k], jnp.broadcast_to(row(X_CH + n + k), row_z.shape), other)
                    return other.astype(jnp.bfloat16)

                value = spread(7, jnp.zeros_like(row_z))
                slope = spread(10, jnp.zeros_like(row_z))
                home = spread(16, jnp.full_like(row_z, -1.0))
                zero = jnp.zeros_like(value)
                for group in range(BZ // PACK):
                    rows = pl.ds(group * PACK, PACK)
                    here = home == jnp.bfloat16(group)
                    val[rows, cols] = jnp.where(here, value, zero)
                    der[rows, cols] = jnp.where(here, slope, zero)

    def multiply(g, buf):
        left, third, val, der = buf
        dims = (((1,), (1,)), ((), ()))
        both = lax.dot_general(left[...], val[...], dims, preferred_element_type=jnp.float32)
        part = lax.dot_general(third[...], der[...], dims, preferred_element_type=jnp.float32)
        half = HALO_X * ROWS_Y
        column = lax.rem(g, n_columns)
        above = jnp.where(column == n_columns - 1, n_columns, column + 1)
        below = jnp.where(column == 0, n_columns, column - 1)
        for f, field in enumerate((both[:half] + part, both[half:])):
            field = field.reshape(HALO_X, ROWS_Y, BZ)
            inner, outer = field[:, :BY], field[:, BY:]
            grid[f, column] += inner
            grid[f, above] += jnp.where(edge == 0, outer, 0.0)
            grid[f, below] += jnp.where(edge == BY - 1, outer, 0.0)

    def stage_refs(f, s, j):
        ref = (starts[f] if s == 0 else sums[f][s - 1]).at[j]
        alive = [k for k in reversed(range(steps)) if k not in orders[f][:s]]
        k = orders[f][s]
        lead = (slice(None),) * alive.index(k)
        return ref, lead, k

    def stage_copy(f, s, j):
        ref, lead, k = stage_refs(f, s, j)
        return pltpu.make_async_remote_copy(
            src_ref=ref.at[lead + (1 - bit_of(k),)],
            dst_ref=got[f][s].at[j],
            send_sem=send_sem.at[f, s, j],
            recv_sem=recv_sem.at[f, s, j],
            device_id=partner(k),
            device_id_type=MESH,
        )

    def cross_copy(kind, j):
        source = (done.at[j, :, pl.ds(1, BX)], done.at[j, :, pl.ds(0, 1)], done.at[j, :, pl.ds(BX + 1, 1)])[kind]
        target = (z_main, z_low, z_high)[kind].at[j]
        owner = lax.rem(me_x + (1, n_slabs, 2)[kind] + j, n_slabs)
        return pltpu.make_async_remote_copy(
            src_ref=source,
            dst_ref=target,
            send_sem=send_z.at[kind, j],
            recv_sem=recv_z.at[kind, j],
            device_id=(owner, me_y),
            device_id_type=MESH,
        )

    at_home = (n_slabs - 1, 0, n_slabs - 2)

    def cross_start(kind, j):
        if isinstance(j, int):
            if j != at_home[kind]:
                cross_copy(kind, j).start()
        else:
            @pl.when(j != at_home[kind])
            def _():
                cross_copy(kind, j).start()

    def event(s, j):
        for f in range(2):
            stage_copy(f, s - 1, j).wait()
            ref, lead, k = stage_refs(f, s - 1, j)
            total = ref[lead + (bit_of(k),)] + got[f][s - 1][j]
            if s == steps:
                done[j, f] = total
            else:
                sums[f][s - 1][j] = total
                stage_copy(f, s, j).start()
        if s == steps:
            for kind in range(3):
                cross_start(kind, j)

    build(0, bufs[0])
    pl.semaphore_wait(barrier, steps + n_slabs - 1)
    pairs = n_columns // 4

    def half_step(h, _):
        step, half = h // 2, lax.rem(h, 2)

        def pair(p, _):
            g = (h * pairs + p) * 2
            build(g + 1, bufs[1])
            multiply(g, bufs[0])
            build(jnp.minimum(g + 2, last), bufs[0])
            multiply(g + 1, bufs[1])
            return 0

        lax.fori_loop(0, pairs, pair, 0)

        @pl.when(half == 1)
        def _():
            for f in range(2):
                for column in range(n_columns):
                    bits = tuple((column >> k) & 1 for k in reversed(range(steps)))
                    starts[f][(step,) + bits] = grid[f, column]
                stage_copy(f, 0, step).start()
            grid[...] = jnp.zeros_like(grid)

        for s in range(1, steps + 1):
            @pl.when((half == (0 if s == 1 else 1)) & (step >= s))
            def _():
                event(s, step - s)

        return 0

    lax.fori_loop(0, 2 * n_slabs, half_step, 0)
    for r in range(1, steps + 1):
        for s in range(r, steps + 1):
            if n_slabs - 1 - (s - r) >= 0:
                event(s, n_slabs - 1 - (s - r))

    main = [done[n_slabs - 1, f, pl.ds(1, BX)] for f in range(2)]
    low = [done[0, f, 0] for f in range(2)]
    high = [done[n_slabs - 2, f, BX + 1] for f in range(2)]
    for j in range(n_slabs):
        for kind in range(3):
            if j != at_home[kind]:
                cross_copy(kind, j).wait()
                for f in range(2):
                    if kind == 0:
                        main[f] = main[f] + z_main[j, f]
                    elif kind == 1:
                        low[f] = low[f] + z_low[j, f, 0]
                    else:
                        high[f] = high[f] + z_high[j, f, 0]
    for f in range(2):
        out = out_ref.at[f]
        out[...] = main[f]
        out[BX - 1] += jnp.where(me_x < n_slabs - 1, low[f], 0.0)
        out[0] += jnp.where(me_x > 0, high[f], 0.0)


def fused(capacity, n_slabs, n_columns, table, off, frac, norm, weight):
    tiles, tile_len = off.shape
    points = capacity * tile_len
    lanes = tile_len
    steps = n_columns.bit_length() - 1
    block = (HALO_X, BY, BZ)
    vmem = pl.BlockSpec(memory_space=pltpu.VMEM)
    smem = pl.BlockSpec(memory_space=pltpu.SMEM)

    def stage(s):
        return pltpu.VMEM((n_slabs,) + (2,) * (steps - s) + block, jnp.float32)

    got = [stage(s + 1) for s in range(steps)]
    sums = [stage(s + 1) for s in range(steps - 1)]
    return pl.pallas_call(
        functools.partial(fused_kernel, capacity, n_slabs, n_columns),
        out_shape=jax.ShapeDtypeStruct((2, BX, BY, BZ), jnp.float32),
        in_specs=[smem, vmem, vmem, vmem, vmem],
        out_specs=vmem,
        scratch_shapes=[pltpu.VMEM((CHANNELS, tile_len // lanes, tiles, lanes), jnp.float32)]
        + [pltpu.VMEM((2 * HALO_X * ROWS_Y, points), jnp.bfloat16)] * 2
        + [pltpu.VMEM((HALO_X * ROWS_Y, points), jnp.bfloat16)] * 2
        + [pltpu.VMEM((BZ, points), jnp.bfloat16)] * 4
        + [
            pltpu.VMEM((2, n_columns + 1) + block, jnp.float32),
            pltpu.VMEM((n_slabs, 2) + block, jnp.float32),
            pltpu.VMEM((n_slabs, 2, BX, BY, BZ), jnp.float32),
            pltpu.VMEM((n_slabs, 2, 1, BY, BZ), jnp.float32),
            pltpu.VMEM((n_slabs, 2, 1, BY, BZ), jnp.float32),
            pltpu.SemaphoreType.DMA((2, steps, n_slabs)),
            pltpu.SemaphoreType.DMA((2, steps, n_slabs)),
            pltpu.SemaphoreType.DMA((3, n_slabs)),
            pltpu.SemaphoreType.DMA((3, n_slabs)),
        ]
        + [stage(0)] * 2 + got * 2 + sums * 2,
        compiler_params=pltpu.CompilerParams(collective_id=0, has_side_effects=True),
        name="fused",
    )(table, off, frac, norm, weight)


def brick_table(capacity, bricks, dest, count):
    tiles = dest.shape[0]
    order = jnp.arange(tiles, dtype=jnp.int32)
    valid = order < count
    earlier = (dest[:, None] == dest[None, :]) & valid[None, :] & (order[None, :] < order[:, None])
    rank = jnp.sum(earlier.astype(jnp.int32), axis=1)
    slot = jnp.where(valid, dest * capacity + rank, -1)
    slots = jnp.arange(bricks * capacity, dtype=jnp.int32)
    found = jnp.where(slots[:, None] == slot[None, :], order[None, :], -1)
    return jnp.max(found, axis=1)


def shards(brick_ids, voxel_offset, fractions, normals, point_weight, tile_count):
    n_slabs = lax.axis_size("gx")
    n_columns = lax.axis_size("yz")
    devices = n_slabs * n_columns
    tiles_here = brick_ids.shape[0]
    capacity = max(2, (tiles_here + devices - 1) // devices)
    table = brick_table(capacity, devices, brick_ids.reshape(tiles_here), tile_count[0])
    both = fused(
        capacity, n_slabs, n_columns, table, voxel_offset,
        jnp.transpose(fractions, (1, 0, 2)), jnp.transpose(normals, (1, 0, 2)), point_weight,
    )
    return (both[0], both[1])


def solution(mesh):
    return jax.shard_map(
        shards,
        mesh=mesh,
        in_specs=(
            P(("gx", "yz"), None),
            P(("gx", "yz"), None),
            P(("gx", "yz"), None, None),
            P(("gx", "yz"), None, None),
            P(("gx", "yz"), None),
            P(("gx", "yz")),
        ),
        out_specs=(P("gx", "yz", None), P("gx", "yz", None)),
        check_vma=False,
    )
```

profile of v0, /device:TPU:0, one launch (start us, length us, event | category | flops | bytes accessed | tf_op | source)
XLA Modules:
  0.0 34.6 jit_solution(13440689004154981174)
XLA Ops:
  1.3 0.0 copy-start
  1.3 0.6 %copy-done = s32[128,1]{0,1:T(1,128)S(1)} copy-done((s32[128,1]{0,1:T(1,128)S(1)}, s32[128,1]{0,1:T(1,128)}, u32[]{:S(2)}) %copy-start) | copy-done | bytes 536
  1.9 0.2 convert_reduce_fusion
  2.1 0.6 %select_reduce_fusion.table_ref = s32[128]{0:T(128)} fusion(s32[128]{0:T(128)S(1)} %add_select_fusion), kind=kLoop, calls=%fused_computation | loop fusion | flops 49024 | bytes 1024 | tf_op jit(solution)/shard_map/reduce_max | solution.py:337
  2.8 30.5 %fused.1 = f32[2,4,8,128]{3,2,1,0:T(8,128)} custom-call(s32[128]{0:T(128)} %select_reduce_fusion.table_ref, s32[128,256]{1,0:T(8,128)} %off_ref.1, f32[3,128,256]{2,1,0:T(8,128)} %bitcast.11, f32[3,128,256]{2,1,0:T(8,128)} %bitcast.12, f32[128,256]{1,0:T(8,128)} %weight_ref.1), custom_call_target="tpu_custom_call" | custom-call | tf_op jit(solution)/shard_map/fused/pallas_call | solution.py:302
  33.2 1.3 %slice_bitcast_fusion = (f32[4,8,128]{2,1,0:T(8,128)}, f32[4,8,128]{2,1,0:T(8,128)}) fusion(f32[2,4,8,128]{3,2,1,0:T(8,128)} %fused.1), kind=kLoop, calls=%fused_computation.5 | loop fusion | bytes 65536 | tf_op jit(solution)/shard_map/squeeze | solution.py:351
  (2 shorter events, 0.0 us)
Async XLA Ops:
  1.3 0.7 %copy-start = (s32[128,1]{0,1:T(1,128)S(1)}, s32[128,1]{0,1:T(1,128)}, u32[]{:S(2)}) copy-start(s32[128,1]{0,1:T(1,128)} %param.6) | copy-start | bytes 1540
where the time goes:
time: 34.8 us; the launch traced here: 34.6 us
  Pallas kernels  30.5 us (88%)
  local copies, waits for them, and re-layouts  1.99 us (6%)
  between operations  1.31 us (4%)
  other arithmetic  0.82 us (2%)
    pallas_call x1, Pallas kernels, fused(): pl.pallas_call(functools.partial(fused_kernel, capacity, n_slabs, n_colum...  30.5 us
    squeeze x1, local copies, waits for them, and re-layouts, shards(): return (both[0], both[1])  1.35 us

commit v1 on v0

v1 whole, which is shorter than its diff:
```python
import functools

import jax
import jax.numpy as jnp
from jax import lax
from jax.experimental import pallas as pl
from jax.experimental.pallas import tpu as pltpu
from jax.sharding import PartitionSpec as P

BX = 4
BY = 8
BZ = 128
MESH = pl.DeviceIdType.MESH
F32, BF16, I32 = jnp.float32, jnp.bfloat16, jnp.int32
LANES = 128
SUB = 8
HALO_X = BX + 2
HALO_Y = BY + 2
ROWS = HALO_Y * SUB
CHUNKS = 2
GROUP = 4
CX, WX, GX, NRM, WGT, YW, YG, WZ, GZ = 0, 1, 4, 7, 10, 11, 11 + HALO_Y, 11 + 2 * HALO_Y, 14 + 2 * HALO_Y
CHANNELS = 17 + 2 * HALO_Y


def spline(frac):
    weights = [0.5 * (1.0 - frac) ** 2, 0.75 - (frac - 0.5) ** 2, 0.5 * frac * frac]
    slopes = [frac - 1.0, 1.0 - 2.0 * frac, frac]
    return (weights, slopes)


def pick(masks, values):
    out = jnp.zeros_like(values[0])
    for mask, value in zip(masks, values):
        out = jnp.where(mask, value, out)
    return out


def twice(value):
    return jnp.concatenate([value, value], axis=0).astype(BF16)


def pair_up(upper, lower):
    return jnp.concatenate([upper, lower], axis=0).astype(BF16)


def prepare(rows, off_ref, frac_ref, norm_ref, weight_ref, chan, cell_z):
    z_bits, y_bits = BZ.bit_length() - 1, BY.bit_length() - 1
    for half in range(chan.shape[0]):
        cols = pl.ds(half * LANES, LANES)

        def keep(n, value):
            chan[half, n, rows, :] = value

        offset = off_ref[rows, cols]
        keep(CX, (offset >> (z_bits + y_bits)).astype(F32))
        cell_z[half, rows, :] = offset & (BZ - 1)
        cell_y = (offset >> z_bits) & (BY - 1)
        wx, gx = spline(frac_ref[0, rows, cols])
        wy, gy = spline(frac_ref[1, rows, cols])
        wz, gz = spline(frac_ref[2, rows, cols])
        for k in range(3):
            keep(WX + k, wx[k])
            keep(GX + k, gx[k])
            keep(NRM + k, norm_ref[k, rows, cols])
            keep(WZ + k, wz[k])
            keep(GZ + k, gz[k])
        keep(WGT, weight_ref[rows, cols])
        at = [cell_y == m for m in range(BY)]
        for y in range(HALO_Y):
            taps = [k for k in range(3) if 0 <= y - k < BY]
            keep(YW + y, pick([at[y - k] for k in taps], [wy[k] for k in taps]))
            keep(YG + y, pick([at[y - k] for k in taps], [gy[k] for k in taps]))


def brick_table(capacity, slots, dest, count):
    tiles = dest.shape[1]
    across = jnp.broadcast_to(dest, (tiles, tiles))
    down = jnp.transpose(across)
    later = lax.broadcasted_iota(I32, (tiles, tiles), 0)
    sooner = lax.broadcasted_iota(I32, (tiles, tiles), 1)
    earlier = (across == down) & (sooner < later) & (sooner < count)
    rank = jnp.sum(jnp.where(earlier, 1, 0), axis=1, keepdims=True)
    tile = lax.broadcasted_iota(I32, (tiles, 1), 0)
    slot = jnp.where(tile < count, down[:, :1] * capacity + rank, -1)
    wanted = lax.broadcasted_iota(I32, (tiles, slots), 1)
    found = jnp.where(slot == wanted, jnp.broadcast_to(tile, (tiles, slots)), -1)
    return jnp.max(found, axis=0, keepdims=True)


def fused_kernel(
    capacity, n_slabs, n_columns, dest_hbm, count_hbm, off_hbm, frac_hbm, norm_hbm, weight_hbm, rhs_ref, screen_ref,
    dest, off, frac, norm, weight, table_v, table, chan, cell_z, grid,
    parts, core_in, mine, peer_in, ready, main_in, low_in, tail_low, tail_high,
    load_sem, core_sem, peer_sem, main_sem, low_sem, tail_sem,
):
    tiles, tile_len = off.shape
    halves = tile_len // LANES
    n_chips = n_columns // 2
    last = n_slabs - 1
    me_x, me_y = lax.axis_index("gx"), lax.axis_index("yz")
    me_c, me_b = me_y // 2, lax.rem(me_y, 2)

    def slab_of(step):
        return lax.rem(me_x + 1 + step, n_slabs)

    def slab_at(hop):
        return lax.rem(me_x + hop + n_slabs, n_slabs)

    def column_at(hop):
        return 2 * lax.rem(me_c + hop, n_chips) + me_b

    loads = [
        pltpu.make_async_copy(dest_hbm, dest, load_sem.at[0]),
    ]
    span = tiles // CHUNKS
    chunks = []
    for n in range(CHUNKS):
        rows = pl.ds(n * span, span)
        base = 3 + 4 * n
        chunks.append([
            pltpu.make_async_copy(off_hbm.at[rows], off.at[rows], load_sem.at[base]),
            pltpu.make_async_copy(frac_hbm.at[:, rows], frac.at[:, rows], load_sem.at[base + 1]),
            pltpu.make_async_copy(norm_hbm.at[:, rows], norm.at[:, rows], load_sem.at[base + 2]),
            pltpu.make_async_copy(weight_hbm.at[rows], weight.at[rows], load_sem.at[base + 3]),
        ])
    for copy in loads + sum(chunks, []):
        copy.start()

    barrier = pltpu.get_barrier_semaphore()
    friends = [(me_x, me_y + 1 - 2 * me_b)]
    friends += [(slab_at(z), column_at(c)) for z in range(n_slabs) for c in range(n_chips) if z or c]
    for friend in friends:
        pl.semaphore_signal(barrier, inc=1, device_id=friend, device_id_type=MESH)

    grid[...] = jnp.zeros_like(grid)

    for copy in loads:
        copy.wait()
    table_v[...] = brick_table(capacity, table_v.shape[1], dest[...], count_hbm[0])

    def prepare_rows(step, _):
        prepare(pl.ds(pl.multiple_of(step * SUB, SUB), SUB), off, frac, norm, weight, chan, cell_z)
        return 0

    table_copy = pltpu.make_async_copy(table_v, table, load_sem.at[2])
    for n in range(CHUNKS):
        for copy in chunks[n]:
            copy.wait()
        if n == CHUNKS - 1:
            table_copy.start()
        lax.fori_loop(n * span // SUB, (n + 1) * span // SUB, prepare_rows, 0)
    table_copy.wait()

    sub = lax.broadcasted_iota(I32, (SUB, LANES), 0)

    def layer_of(slab):
        return (sub + 4 * lax.rem(slab, 2)) & (SUB - 1)

    def brick_sum(g):
        slab = slab_of(g // n_columns)
        brick = slab * n_columns + lax.rem(g, n_columns)
        layer = layer_of(slab)
        outside = ((layer == 0) & (slab == 0)) | ((layer == HALO_X - 1) & (slab == last))
        layer = jnp.where(outside, -SUB, layer).astype(F32)
        out = None
        for c in range(capacity):
            lefts, rights = [], []
            entry = table[0, brick * capacity + c]
            away = jnp.where(entry >= 0, 0.0, 8.0 * SUB)
            tile = jnp.minimum(jnp.maximum(entry, 0), tiles - 1)
            for half in range(halves):
                left, right = [[], [], []], [[], []]

                def row(n):
                    return jnp.broadcast_to(chan[half, n, pl.ds(tile, 1), :], (SUB, LANES))

                gap = layer - (row(CX) + away)
                hit = [gap == float(k) for k in range(3)]
                wx = pick(hit, [row(WX + k) for k in range(3)])
                gx = pick(hit, [row(GX + k) for k in range(3)])
                first, second = gx * row(NRM), wx * row(NRM + 1)
                third, plain = twice(wx * row(NRM + 2)), twice(wx * row(WGT))
                for m in range(HALO_Y // 2):
                    wy = [row(YW + 2 * m), row(YW + 2 * m + 1)]
                    gy = [row(YG + 2 * m), row(YG + 2 * m + 1)]
                    both = pair_up(first * wy[0] + second * gy[0], first * wy[1] + second * gy[1])
                    wide = pair_up(wy[0], wy[1])
                    left[0].append(both)
                    left[1].append(plain * wide)
                    left[2].append(third * wide)
                z = jnp.broadcast_to(cell_z[half, pl.ds(tile, 1), :], (SUB, LANES))
                tap = (sub - z + 1) & (SUB - 1)
                hit = [tap == k for k in range(3)]
                value = twice(pick(hit, [row(WZ + k) for k in range(3)]))
                slope = twice(pick(hit, [row(GZ + k) for k in range(3)]))
                home = ((z - 1 + tap) >> 3).astype(F32)
                home = pair_up(home, home - 1.0)
                zero = jnp.zeros_like(value)
                for m in range(BZ // (2 * SUB)):
                    here = home == jnp.bfloat16(2 * m)
                    right[0].append(jnp.where(here, value, zero))
                    right[1].append(jnp.where(here, slope, zero))
                lefts.append(jnp.concatenate(sum(left, []), axis=0))
                rights.append(jnp.concatenate(sum(right, []), axis=0))
            dims = (((1,), (1,)), ((), ()))
            more = lax.dot_general(
                jnp.concatenate(lefts, axis=1), jnp.concatenate(rights, axis=1), dims, preferred_element_type=F32
            )
            out = more if out is None else out + more
        return out

    def add_brick(g):
        out = brick_sum(g)
        rhs = out[:ROWS, :BZ] + out[2 * ROWS :, BZ:]
        screen = out[ROWS : 2 * ROWS, :BZ]
        step, column = g // n_columns, lax.rem(g, n_columns)
        carried = (layer_of(slab_of(step)) < 2) & (step > 0)
        edge = carried | (column > 0)
        for f, field in enumerate((rhs, screen)):
            for y in range(HALO_Y):
                at = pl.ds(pl.multiple_of((column * BY + y) * SUB, SUB), SUB)
                old = jnp.where(edge if y < 2 else carried, grid[f, at, :], 0.0)
                grid[f, at, :] = field[y * SUB : (y + 1) * SUB] + old

    def core_copy(j):
        layers = pl.ds(0, HALO_X if j == last else BX)
        return pltpu.make_async_remote_copy(
            src_ref=parts.at[j, 1 - me_b, :, layers],
            dst_ref=core_in.at[j, :, layers],
            send_sem=core_sem.at[0, j],
            recv_sem=core_sem.at[1, j],
            device_id=(me_x, me_y + 1 - 2 * me_b),
            device_id_type=MESH,
        )

    def peer_copy(j, hop):
        return pltpu.make_async_remote_copy(
            src_ref=mine.at[j, lax.rem(me_c + hop, n_chips), pl.ds(1 if j == last else 0, BX)],
            dst_ref=peer_in.at[j, hop],
            send_sem=peer_sem.at[0, j, hop],
            recv_sem=peer_sem.at[1, j, hop],
            device_id=(me_x, column_at(hop)),
            device_id_type=MESH,
        )

    def main_copy(j):
        return pltpu.make_async_remote_copy(
            src_ref=ready.at[j, pl.ds(1, BX - 1)],
            dst_ref=main_in.at[j],
            send_sem=main_sem.at[0, j],
            recv_sem=main_sem.at[1, j],
            device_id=(slab_at(1 + j), me_y),
            device_id_type=MESH,
        )

    def low_copy(j):
        return pltpu.make_async_remote_copy(
            src_ref=ready.at[j, 0],
            dst_ref=low_in.at[j],
            send_sem=low_sem.at[0, j],
            recv_sem=low_sem.at[1, j],
            device_id=(slab_at(j), me_y),
            device_id_type=MESH,
        )

    def tail_copy(side, hop):
        layer, target, to = ((0, tail_low, -1), (HALO_X - 1, tail_high, 1))[side]
        return pltpu.make_async_remote_copy(
            src_ref=mine.at[last, lax.rem(me_c + hop, n_chips), layer],
            dst_ref=target.at[hop],
            send_sem=tail_sem.at[0, side, hop],
            recv_sem=tail_sem.at[1, side, hop],
            device_id=(slab_at(to), column_at(hop)),
            device_id_type=MESH,
        )

    def share(j):
        start = 4 * lax.rem(slab_of(j), 2)
        for layer in range(HALO_X if j == last else BX):
            at = lax.rem(start + layer, SUB)
            for column in range(n_columns):
                for f in range(2):
                    rows = pl.ds((column * BY + 1) * SUB + at, BY, stride=SUB)
                    parts[j, column % 2, column // 2, layer, f] = grid[f, rows, :]
        core_copy(j).start()

    def spread(j):
        core_copy(j).wait()
        for chip in range(n_chips):
            for layer in range(HALO_X if j == last else BX):
                mine[j, chip, layer] = parts[j, me_b, chip, layer] + core_in[j, chip, layer]
        for hop in range(1, n_chips):
            peer_copy(j, hop).start()
        if j == last:
            for hop in range(n_chips):
                tail_copy(0, hop).start()

            @pl.when(me_x < last)
            def _():
                for hop in range(n_chips):
                    tail_copy(1, hop).start()

    def forward(j):
        for hop in range(1, n_chips):
            peer_copy(j, hop).wait()
        for layer in range(BX):
            total = mine[j, me_c, layer]
            for hop in range(1, n_chips):
                total = total + peer_in[j, hop, layer]
            ready[j, layer] = total
        main_copy(j).start()
        if j > 0:
            low_copy(j).start()

    group = min(GROUP, n_columns)
    turns = n_columns // group
    pl.semaphore_wait(barrier, len(friends))
    for step in range(n_slabs):

        def turn(p, _):
            for k in range(group):
                add_brick(step * n_columns + p * group + k)
            if step > 0:
                @pl.when(p == max(0, turns - 2))
                def _():
                    spread(step - 1)

            return 0

        lax.fori_loop(0, turns, turn, 0)
        share(step)
    early = n_slabs - 2
    for j in range(0, max(0, early - 1)):
        forward(j)
    spread(last)
    for j in range(max(0, early - 1), last):
        forward(j)

    outs = (rhs_ref, screen_ref)
    for j in range(last):
        main_copy(j).wait()
        if j > 0:
            low_copy(j).wait()
    for hop in range(1, n_chips):
        peer_copy(last, hop).wait()
    for hop in range(n_chips):
        tail_copy(0, hop).wait()
    for layer in range(BX):
        total = mine[last, me_c, layer + 1]
        for hop in range(1, n_chips):
            total = total + peer_in[last, hop, layer]
        if layer < BX - 1:
            for j in range(last):
                total = total + main_in[j, layer]
        else:
            total = total + ready[0, 0]
            for j in range(1, last):
                total = total + low_in[j]
            for hop in range(n_chips):
                total = total + tail_low[hop]
        for f in range(2):
            outs[f][layer] = total[f]

    @pl.when(me_x < last)
    def _():
        for hop in range(n_chips):
            tail_copy(1, hop).wait_send()

    @pl.when(me_x > 0)
    def _():
        for hop in range(n_chips):
            tail_copy(1, hop).wait_recv()
        for f in range(2):
            total = outs[f][0]
            for hop in range(n_chips):
                total = total + tail_high[hop, f]
            outs[f][0] = total


def fused(capacity, n_slabs, n_columns, dest, count, off, frac, norm, weight):
    tiles, tile_len = off.shape
    slots = n_slabs * n_columns * capacity
    n_chips = n_columns // 2
    block = (2, BY, BZ)
    dma = pltpu.SemaphoreType.DMA
    out = jax.ShapeDtypeStruct((BX, BY, BZ), F32)
    return pl.pallas_call(
        functools.partial(fused_kernel, capacity, n_slabs, n_columns),
        out_shape=(out, out),
        in_specs=[pl.BlockSpec(memory_space=pltpu.HBM), pl.BlockSpec(memory_space=pltpu.SMEM)] + [pl.BlockSpec(memory_space=pltpu.HBM)] * 4,
        out_specs=(pl.BlockSpec(memory_space=pltpu.VMEM),) * 2,
        scratch_shapes=[
            pltpu.VMEM((1, tiles), I32),
            pltpu.VMEM((tiles, tile_len), I32),
            pltpu.VMEM((3, tiles, tile_len), F32),
            pltpu.VMEM((3, tiles, tile_len), F32),
            pltpu.VMEM((tiles, tile_len), F32),
            pltpu.VMEM((1, slots), I32),
            pltpu.SMEM((1, slots), I32),
            pltpu.VMEM((tile_len // LANES, CHANNELS, tiles + SUB, LANES), F32),
            pltpu.VMEM((tile_len // LANES, tiles, LANES), I32),
            pltpu.VMEM((2, (n_columns * BY + 2) * SUB, BZ), F32),
            pltpu.VMEM((n_slabs, 2, n_chips, HALO_X) + block, F32),
            pltpu.VMEM((n_slabs, n_chips, HALO_X) + block, F32),
            pltpu.VMEM((n_slabs, n_chips, HALO_X) + block, F32),
            pltpu.VMEM((n_slabs, n_chips, BX) + block, F32),
            pltpu.VMEM((n_slabs, BX) + block, F32),
            pltpu.VMEM((n_slabs, BX - 1) + block, F32),
            pltpu.VMEM((n_slabs,) + block, F32),
            pltpu.VMEM((n_chips,) + block, F32),
            pltpu.VMEM((n_chips,) + block, F32),
            dma((3 + 4 * CHUNKS,)),
            dma((2, n_slabs)),
            dma((2, n_slabs, n_chips)),
            dma((2, n_slabs)),
            dma((2, n_slabs)),
            dma((2, 2, n_chips)),
        ],
        compiler_params=pltpu.CompilerParams(collective_id=0, has_side_effects=True),
        name="fused",
    )(dest, count, off, frac, norm, weight)


def shards(brick_ids, voxel_offset, fractions, normals, point_weight, tile_count):
    n_slabs = lax.axis_size("gx")
    n_columns = lax.axis_size("yz")
    devices = n_slabs * n_columns
    tiles_here = brick_ids.shape[0]
    capacity = max(2, (tiles_here + devices - 1) // devices)
    return fused(
        capacity, n_slabs, n_columns, brick_ids.reshape(1, tiles_here), tile_count, voxel_offset,
        jnp.transpose(fractions, (1, 0, 2)), jnp.transpose(normals, (1, 0, 2)), point_weight,
    )


def solution(mesh):
    return jax.shard_map(
        shards,
        mesh=mesh,
        in_specs=(
            P(("gx", "yz"), None),
            P(("gx", "yz"), None),
            P(("gx", "yz"), None, None),
            P(("gx", "yz"), None, None),
            P(("gx", "yz"), None),
            P(("gx", "yz")),
        ),
        out_specs=(P("gx", "yz", None), P("gx", "yz", None)),
        check_vma=False,
    )
```

time: 34.8 us -> 25.4 us (0.73)
  Pallas kernels: 30.5 us -> 21.9 us
  other arithmetic: 0.82 us -> 0 us
    pallas_call x1, Pallas kernels: 30.5 us -> 21.9 us  [fused(): pl.pallas_call(functools.partial(fused_kernel, capacity, n_slabs, n_colum...]
    squeeze x1 -> x0, local copies, waits for them, and re-layouts: 1.35 us -> none  [shards(): return (both[0], both[1])]
    unnamed x2 -> x4, local copies, waits for them, and re-layouts: 0.64 us -> 1.94 us
    reduce_max x1 -> x0, other arithmetic: 0.63 us -> none  [brick_table(): return jnp.max(found, axis=1)]
where the time goes in v1:
time: 25.4 us; the launch traced here: 25.2 us
  Pallas kernels  21.9 us (86%)
  local copies, waits for them, and re-layouts  1.94 us (8%)
  between operations  1.29 us (5%)
    pallas_call x1, Pallas kernels, fused(): pl.pallas_call(functools.partial(fused_kernel, capacity, n_slabs, n_colum...  21.9 us
    unnamed x4, local copies, waits for them, and re-layouts  1.94 us

profile of v1, /device:TPU:0, one launch (start us, length us, event | category | flops | bytes accessed | tf_op | source)
XLA Modules:
  0.0 25.2 jit_solution(7752183159451727190)
XLA Ops:
  1.3 21.9 %fused.1 = (f32[4,8,128]{2,1,0:T(8,128)}, f32[4,8,128]{2,1,0:T(8,128)}) custom-call(s32[1,128]{1,0:T(1,128)} %bitcast.5, s32[1]{0:T(128)S(6)} %copy.10.count_hbm, s32[128,256]{1,0:T(8,128)} %off_hbm.1, f32[3,128,256]{2,1,0:T(8,128)} %bitcast.3, f32[3,128,256]{2,1,0:T(8,128)} %bitcast.4, f32[128,256]{1,0:T(8,128)} %weight_hbm.1), custom_call_target="tpu_custom_call" | custom-call | tf_op jit(solution)/shard_map/fused/pallas_call | solution.py:388
  23.2 0.0 copy-start
  23.2 1.3 %copy.11 = f32[4,8,128]{2,1,0:T(8,128)} copy(f32[4,8,128]{2,1,0:T(8,128)} %get-tuple-element.4) | data formatting | bytes 32768
  24.6 0.0 copy-done
  24.6 0.6 %copy.12 = f32[4,8,128]{2,1,0:T(8,128)} copy(f32[4,8,128]{2,1,0:T(8,128)S(1)} %copy-done) | data formatting | bytes 32768
Async XLA Ops:
  23.2 1.3 %copy-start = (f32[4,8,128]{2,1,0:T(8,128)S(1)}, f32[4,8,128]{2,1,0:T(8,128)}, u32[]{:S(2)}) copy-start(f32[4,8,128]{2,1,0:T(8,128)} %get-tuple-element.5) | copy-start | bytes 49156

commit v2 on v1

--- a/solution.py
+++ b/solution.py
@@ -18,7 +18,6 @@
 HALO_Y = BY + 2
 ROWS = HALO_Y * SUB
 CHUNKS = 2
-GROUP = 4
 CX, WX, GX, NRM, WGT, YW, YG, WZ, GZ = 0, 1, 4, 7, 10, 11, 11 + HALO_Y, 11 + 2 * HALO_Y, 14 + 2 * HALO_Y
 CHANNELS = 17 + 2 * HALO_Y
 
@@ -89,7 +88,7 @@
 
 
 def fused_kernel(
-    capacity, n_slabs, n_columns, dest_hbm, count_hbm, off_hbm, frac_hbm, norm_hbm, weight_hbm, rhs_ref, screen_ref,
+    capacity, n_slabs, n_columns, dest_hbm, count_hbm, off_hbm, frac_hbm, norm_hbm, weight_hbm, out_ref,
     dest, off, frac, norm, weight, table_v, table, chan, cell_z, grid,
     parts, core_in, mine, peer_in, ready, main_in, low_in, tail_low, tail_high,
     load_sem, core_sem, peer_sem, main_sem, low_sem, tail_sem,
@@ -97,9 +96,12 @@
     tiles, tile_len = off.shape
     halves = tile_len // LANES
     n_chips = n_columns // 2
+    near = n_chips // 2
     last = n_slabs - 1
     me_x, me_y = lax.axis_index("gx"), lax.axis_index("yz")
     me_c, me_b = me_y // 2, lax.rem(me_y, 2)
+    me_h, me_r = me_c // near, lax.rem(me_c, near)
+    first_column = (n_columns // 2 - 1) * (1 - me_h)
 
     def slab_of(step):
         return lax.rem(me_x + 1 + step, n_slabs)
@@ -109,6 +111,15 @@
 
     def column_at(hop):
         return 2 * lax.rem(me_c + hop, n_chips) + me_b
+
+    def half_at(part):
+        return lax.rem(me_h + 1 + part, 2)
+
+    def place(part, turn):
+        return lax.rem(me_r + turn, near)
+
+    def hop_to(part, turn):
+        return lax.rem(half_at(part) * near + place(part, turn) - me_c + n_chips, n_chips)
 
     loads = [
         pltpu.make_async_copy(dest_hbm, dest, load_sem.at[0]),
@@ -157,9 +168,9 @@
     def layer_of(slab):
         return (sub + 4 * lax.rem(slab, 2)) & (SUB - 1)
 
-    def brick_sum(g):
-        slab = slab_of(g // n_columns)
-        brick = slab * n_columns + lax.rem(g, n_columns)
+    def brick_sum(step, column):
+        slab = slab_of(step)
+        brick = slab * n_columns + column
         layer = layer_of(slab)
         outside = ((layer == 0) & (slab == 0)) | ((layer == HALO_X - 1) & (slab == last))
         layer = jnp.where(outside, -SUB, layer).astype(F32)
@@ -210,39 +221,47 @@
             out = more if out is None else out + more
         return out
 
-    def add_brick(g):
-        out = brick_sum(g)
+    def add_brick(step, k):
+        column = lax.rem(first_column + k, n_columns)
+        out = brick_sum(step, column)
         rhs = out[:ROWS, :BZ] + out[2 * ROWS :, BZ:]
         screen = out[ROWS : 2 * ROWS, :BZ]
-        step, column = g // n_columns, lax.rem(g, n_columns)
         carried = (layer_of(slab_of(step)) < 2) & (step > 0)
-        edge = carried | (column > 0)
+        below = carried | (column > 0) if k > 0 else carried
+        above = carried | (first_column > 0) if k == n_columns - 1 else carried
         for f, field in enumerate((rhs, screen)):
             for y in range(HALO_Y):
                 at = pl.ds(pl.multiple_of((column * BY + y) * SUB, SUB), SUB)
-                old = jnp.where(edge if y < 2 else carried, grid[f, at, :], 0.0)
+                keep = below if y < 2 else above if y >= BY else carried
+                old = jnp.where(keep, grid[f, at, :], 0.0)
                 grid[f, at, :] = field[y * SUB : (y + 1) * SUB] + old
 
-    def core_copy(j):
-        layers = pl.ds(0, HALO_X if j == last else BX)
+    def depth(j):
+        return HALO_X if isinstance(j, int) and j == last else BX
+
+    def core_copy(j, part):
+        layers = pl.ds(0, depth(j))
         return pltpu.make_async_remote_copy(
-            src_ref=parts.at[j, 1 - me_b, :, layers],
-            dst_ref=core_in.at[j, :, layers],
-            send_sem=core_sem.at[0, j],
-            recv_sem=core_sem.at[1, j],
+            src_ref=parts.at[j, part, 1 - me_b, :, layers],
+            dst_ref=core_in.at[j, part, :, layers],
+            send_sem=core_sem.at[0, j, part],
+            recv_sem=core_sem.at[1, j, part],
             device_id=(me_x, me_y + 1 - 2 * me_b),
             device_id_type=MESH,
         )
 
-    def peer_copy(j, hop):
+    def peer_copy(j, part, turn):
+        hop = hop_to(part, turn)
         return pltpu.make_async_remote_copy(
-            src_ref=mine.at[j, lax.rem(me_c + hop, n_chips), pl.ds(1 if j == last else 0, BX)],
+            src_ref=mine.at[j, part, place(part, turn), pl.ds(depth(j) - BX - (depth(j) > BX), BX)],
             dst_ref=peer_in.at[j, hop],
             send_sem=peer_sem.at[0, j, hop],
             recv_sem=peer_sem.at[1, j, hop],
             device_id=(me_x, column_at(hop)),
             device_id_type=MESH,
         )
+
+    peers = [(part, turn) for part in range(2) for turn in range(near) if (part, turn) != (1, 0)]
 
     def main_copy(j):
         return pltpu.make_async_remote_copy(
@@ -264,10 +283,11 @@
             device_id_type=MESH,
         )
 
-    def tail_copy(side, hop):
+    def tail_copy(side, part, turn):
         layer, target, to = ((0, tail_low, -1), (HALO_X - 1, tail_high, 1))[side]
+        hop = hop_to(part, turn)
         return pltpu.make_async_remote_copy(
-            src_ref=mine.at[last, lax.rem(me_c + hop, n_chips), layer],
+            src_ref=mine.at[last, part, place(part, turn), layer],
             dst_ref=target.at[hop],
             send_sem=tail_sem.at[0, side, hop],
             recv_sem=tail_sem.at[1, side, hop],
@@ -275,37 +295,38 @@
             device_id_type=MESH,
         )
 
-    def share(j):
+    def share(j, part):
         start = 4 * lax.rem(slab_of(j), 2)
-        for layer in range(HALO_X if j == last else BX):
+        base = half_at(part) * (n_columns // 2)
+        for layer in range(depth(j)):
             at = lax.rem(start + layer, SUB)
-            for column in range(n_columns):
+            for k in range(n_columns // 2):
                 for f in range(2):
-                    rows = pl.ds((column * BY + 1) * SUB + at, BY, stride=SUB)
-                    parts[j, column % 2, column // 2, layer, f] = grid[f, rows, :]
-        core_copy(j).start()
-
-    def spread(j):
-        core_copy(j).wait()
-        for chip in range(n_chips):
-            for layer in range(HALO_X if j == last else BX):
-                mine[j, chip, layer] = parts[j, me_b, chip, layer] + core_in[j, chip, layer]
-        for hop in range(1, n_chips):
-            peer_copy(j, hop).start()
-        if j == last:
-            for hop in range(n_chips):
-                tail_copy(0, hop).start()
+                    rows = pl.ds(((base + k) * BY + 1) * SUB + at, BY, stride=SUB)
+                    parts[j, part, k % 2, k // 2, layer, f] = grid[f, rows, :]
+        core_copy(j, part).start()
+
+    def spread(j, part):
+        core_copy(j, part).wait()
+        for chip in range(near):
+            for layer in range(depth(j)):
+                mine[j, part, chip, layer] = parts[j, part, me_b, chip, layer] + core_in[j, part, chip, layer]
+        for turn in range(part, near):
+            peer_copy(j, part, turn).start()
+        if depth(j) > BX:
+            for turn in range(near):
+                tail_copy(0, part, turn).start()
 
             @pl.when(me_x < last)
             def _():
-                for hop in range(n_chips):
-                    tail_copy(1, hop).start()
+                for turn in range(near):
+                    tail_copy(1, part, turn).start()
 
     def forward(j):
-        for hop in range(1, n_chips):
-            peer_copy(j, hop).wait()
+        for peer in peers:
+            peer_copy(j, *peer).wait()
         for layer in range(BX):
-            total = mine[j, me_c, layer]
+            total = mine[j, 1, me_r, layer]
             for hop in range(1, n_chips):
                 total = total + peer_in[j, hop, layer]
             ready[j, layer] = total
@@ -313,41 +334,51 @@
         if j > 0:
             low_copy(j).start()
 
-    group = min(GROUP, n_columns)
-    turns = n_columns // group
-    pl.semaphore_wait(barrier, len(friends))
-    for step in range(n_slabs):
-
-        def turn(p, _):
-            for k in range(group):
-                add_brick(step * n_columns + p * group + k)
-            if step > 0:
-                @pl.when(p == max(0, turns - 2))
-                def _():
-                    spread(step - 1)
-
-            return 0
-
-        lax.fori_loop(0, turns, turn, 0)
-        share(step)
-    early = n_slabs - 2
-    for j in range(0, max(0, early - 1)):
+    split = n_columns // 2 + 1
+
+    def slab_step(step, first):
+        for k in range(split):
+            add_brick(step, k)
+        if first is None:
+            spread(step - 1, 1)
+        else:
+            first()
+        share(step, 0)
+        for k in range(split, n_columns):
+            add_brick(step, k)
+        share(step, 1)
+        spread(step, 0)
+
+    def early_step(step, _):
+        def first():
+            @pl.when(step == 0)
+            def _():
+                pl.semaphore_wait(barrier, len(friends))
+
+            @pl.when(step > 0)
+            def _():
+                spread(step - 1, 1)
+
+        slab_step(step, first)
+        return 0
+
+    lax.fori_loop(0, last, early_step, 0)
+    slab_step(last, None)
+    spread(last, 1)
+    for j in range(last):
         forward(j)
-    spread(last)
-    for j in range(max(0, early - 1), last):
-        forward(j)
-
-    outs = (rhs_ref, screen_ref)
+
     for j in range(last):
         main_copy(j).wait()
         if j > 0:
             low_copy(j).wait()
-    for hop in range(1, n_chips):
-        peer_copy(last, hop).wait()
-    for hop in range(n_chips):
-        tail_copy(0, hop).wait()
+    for peer in peers:
+        peer_copy(last, *peer).wait()
+    ends = [(part, turn) for part in range(2) for turn in range(near)]
+    for end in ends:
+        tail_copy(0, *end).wait()
     for layer in range(BX):
-        total = mine[last, me_c, layer + 1]
+        total = mine[last, 1, me_r, layer + 1]
         for hop in range(1, n_chips):
             total = total + peer_in[last, hop, layer]
         if layer < BX - 1:
@@ -360,22 +391,26 @@
             for hop in range(n_chips):
                 total = total + tail_low[hop]
         for f in range(2):
-            outs[f][layer] = total[f]
+            out_ref[f, layer] = total[f]
 
     @pl.when(me_x < last)
     def _():
-        for hop in range(n_chips):
-            tail_copy(1, hop).wait_send()
+        for end in ends:
+            tail_copy(1, *end).wait_send()
 
     @pl.when(me_x > 0)
     def _():
-        for hop in range(n_chips):
-            tail_copy(1, hop).wait_recv()
+        for end in ends:
+            tail_copy(1, *end).wait_recv()
         for f in range(2):
-            total = outs[f][0]
+            total = out_ref[f, 0]
             for hop in range(n_chips):
                 total = total + tail_high[hop, f]
-            outs[f][0] = total
+            out_ref[f, 0] = total
+
+
+def hbm(array):
+    return pltpu.with_memory_space_constraint(array, pltpu.HBM)
 
 
 def fused(capacity, n_slabs, n_columns, dest, count, off, frac, norm, weight):
@@ -384,12 +419,12 @@
     n_chips = n_columns // 2
     block = (2, BY, BZ)
     dma = pltpu.SemaphoreType.DMA
-    out = jax.ShapeDtypeStruct((BX, BY, BZ), F32)
+    near = n_chips // 2
     return pl.pallas_call(
         functools.partial(fused_kernel, capacity, n_slabs, n_columns),
-        out_shape=(out, out),
+        out_shape=jax.ShapeDtypeStruct((2, BX, BY, BZ), F32),
         in_specs=[pl.BlockSpec(memory_space=pltpu.HBM), pl.BlockSpec(memory_space=pltpu.SMEM)] + [pl.BlockSpec(memory_space=pltpu.HBM)] * 4,
-        out_specs=(pl.BlockSpec(memory_space=pltpu.VMEM),) * 2,
+        out_specs=pl.BlockSpec(memory_space=pltpu.VMEM),
         scratch_shapes=[
             pltpu.VMEM((1, tiles), I32),
             pltpu.VMEM((tiles, tile_len), I32),
@@ -401,9 +436,9 @@
             pltpu.VMEM((tile_len // LANES, CHANNELS, tiles + SUB, LANES), F32),
             pltpu.VMEM((tile_len // LANES, tiles, LANES), I32),
             pltpu.VMEM((2, (n_columns * BY + 2) * SUB, BZ), F32),
-            pltpu.VMEM((n_slabs, 2, n_chips, HALO_X) + block, F32),
-            pltpu.VMEM((n_slabs, n_chips, HALO_X) + block, F32),
-            pltpu.VMEM((n_slabs, n_chips, HALO_X) + block, F32),
+            pltpu.VMEM((n_slabs, 2, 2, near, HALO_X) + block, F32),
+            pltpu.VMEM((n_slabs, 2, near, HALO_X) + block, F32),
+            pltpu.VMEM((n_slabs, 2, near, HALO_X) + block, F32),
             pltpu.VMEM((n_slabs, n_chips, BX) + block, F32),
             pltpu.VMEM((n_slabs, BX) + block, F32),
             pltpu.VMEM((n_slabs, BX - 1) + block, F32),
@@ -411,15 +446,15 @@
             pltpu.VMEM((n_chips,) + block, F32),
             pltpu.VMEM((n_chips,) + block, F32),
             dma((3 + 4 * CHUNKS,)),
-            dma((2, n_slabs)),
+            dma((2, n_slabs, 2)),
             dma((2, n_slabs, n_chips)),
             dma((2, n_slabs)),
             dma((2, n_slabs)),
             dma((2, 2, n_chips)),
         ],
-        compiler_params=pltpu.CompilerParams(collective_id=0, has_side_effects=True),
+        compiler_params=pltpu.CompilerParams(collective_id=0, has_side_effects=True, vmem_limit_bytes=32 << 20),
         name="fused",
-    )(dest, count, off, frac, norm, weight)
+    )(hbm(dest), count, hbm(off), hbm(frac), hbm(norm), hbm(weight))
 
 
 def shards(brick_ids, voxel_offset, fractions, normals, point_weight, tile_count):
@@ -428,10 +463,11 @@
     devices = n_slabs * n_columns
     tiles_here = brick_ids.shape[0]
     capacity = max(2, (tiles_here + devices - 1) // devices)
-    return fused(
+    both = fused(
         capacity, n_slabs, n_columns, brick_ids.reshape(1, tiles_here), tile_count, voxel_offset,
         jnp.transpose(fractions, (1, 0, 2)), jnp.transpose(normals, (1, 0, 2)), point_weight,
     )
+    return (both[0], both[1])
 
 
 def solution(mesh):

time: 25.4 us -> 23.1 us (0.909)
  local copies, waits for them, and re-layouts: 1.94 us -> 0.61 us
  Pallas kernels: 21.9 us -> 21 us
    unnamed x4 -> x0, local copies, waits for them, and re-layouts: 1.94 us -> none
    pallas_call x1, Pallas kernels: 21.9 us -> 21 us  [fused(): pl.pallas_call(functools.partial(fused_kernel, capacity, n_slabs, n_colum...]
    squeeze x0 -> x1, local copies, waits for them, and re-layouts: none -> 0.61 us  [shards(): return (both[0], both[1])]
where the time goes in v2:
time: 23.1 us; the launch traced here: 22.9 us
  Pallas kernels  21 us (91%)
  between operations  1.29 us (6%)
  local copies, waits for them, and re-layouts  0.61 us (3%)
    pallas_call x1, Pallas kernels, fused(): pl.pallas_call(functools.partial(fused_kernel, capacity, n_slabs, n_colum...  21 us
    squeeze x1, local copies, waits for them, and re-layouts, shards(): return (both[0], both[1])  0.61 us

profile of v2, /device:TPU:0, one launch (start us, length us, event | category | flops | bytes accessed | tf_op | source)
XLA Modules:
  0.0 22.9 jit_solution(18262552443198718508)
XLA Ops:
  1.3 21.0 %fused.1 = f32[2,4,8,128]{3,2,1,0:T(8,128)S(1)} custom-call(s32[1,128]{1,0:T(1,128)} %bitcast.9, s32[1]{0:T(128)S(6)} %copy.8.count_hbm, s32[128,256]{1,0:T(8,128)} %off_hbm.1, f32[3,128,256]{2,1,0:T(8,128)} %bitcast.7, f32[3,128,256]{2,1,0:T(8,128)} %bitcast.8, f32[128,256]{1,0:T(8,128)} %weight_hbm.1), custom_call_target="tpu_custom_call" | custom-call | tf_op jit(solution)/shard_map/fused/pallas_call | solution.py:423
  22.3 0.6 %slice_bitcast_fusion = (f32[4,8,128]{2,1,0:T(8,128)}, f32[4,8,128]{2,1,0:T(8,128)}) fusion(f32[2,4,8,128]{3,2,1,0:T(8,128)S(1)} %fused.1), kind=kLoop, calls=%fused_computation | loop fusion | bytes 65536 | tf_op jit(solution)/shard_map/squeeze | solution.py:470

commit v3 on v2

--- a/solution.py
+++ b/solution.py
@@ -155,12 +155,16 @@
         return 0
 
     table_copy = pltpu.make_async_copy(table_v, table, load_sem.at[2])
+    lead = 1
     for n in range(CHUNKS):
         for copy in chunks[n]:
             copy.wait()
-        if n == CHUNKS - 1:
+        begin, end = n * span // SUB, (n + 1) * span // SUB
+        if n == 0:
+            lax.fori_loop(begin, begin + lead, prepare_rows, 0)
             table_copy.start()
-        lax.fori_loop(n * span // SUB, (n + 1) * span // SUB, prepare_rows, 0)
+            begin = begin + lead
+        lax.fori_loop(begin, end, prepare_rows, 0)
     table_copy.wait()
 
     sub = lax.broadcasted_iota(I32, (SUB, LANES), 0)
@@ -336,38 +340,42 @@
 
     split = n_columns // 2 + 1
 
-    def slab_step(step, first):
+    def early_step(step, _):
+        for k in range(n_columns):
+            add_brick(step, k)
+
+        @pl.when(step == 0)
+        def _():
+            pl.semaphore_wait(barrier, len(friends))
+
+        @pl.when(step > 0)
+        def _():
+            for part in range(2):
+                spread(step - 1, part)
+
+        for part in range(2):
+            share(step, part)
+        return 0
+
+    lax.fori_loop(0, last - 1, early_step, 0)
+    for step in (last - 1, last):
         for k in range(split):
             add_brick(step, k)
-        if first is None:
-            spread(step - 1, 1)
-        else:
-            first()
+        if step < last:
+            spread(step - 1, 0)
+        spread(step - 1, 1)
+        if step == last:
+            for j in range(last - 2):
+                forward(j)
         share(step, 0)
         for k in range(split, n_columns):
             add_brick(step, k)
         share(step, 1)
         spread(step, 0)
-
-    def early_step(step, _):
-        def first():
-            @pl.when(step == 0)
-            def _():
-                pl.semaphore_wait(barrier, len(friends))
-
-            @pl.when(step > 0)
-            def _():
-                spread(step - 1, 1)
-
-        slab_step(step, first)
-        return 0
-
-    lax.fori_loop(0, last, early_step, 0)
-    slab_step(last, None)
+    for j in range(max(0, last - 2), last - 1):
+        forward(j)
     spread(last, 1)
-    for j in range(last):
-        forward(j)
-
+    forward(last - 1)
     for j in range(last):
         main_copy(j).wait()
         if j > 0:

time: 23.1 us -> 21.3 us (0.922)
  Pallas kernels: 21 us -> 19.2 us
    pallas_call x1, Pallas kernels: 21 us -> 19.2 us  [fused(): pl.pallas_call(functools.partial(fused_kernel, capacity, n_slabs, n_colum...]
where the time goes in v3:
time: 21.3 us; the launch traced here: 21.1 us
  Pallas kernels  19.2 us (90%)
  between operations  1.29 us (6%)
  local copies, waits for them, and re-layouts  0.61 us (3%)
    pallas_call x1, Pallas kernels, fused(): pl.pallas_call(functools.partial(fused_kernel, capacity, n_slabs, n_colum...  19.2 us
    squeeze x1, local copies, waits for them, and re-layouts, shards(): return (both[0], both[1])  0.61 us

profile of v3, /device:TPU:0, one launch (start us, length us, event | category | flops | bytes accessed | tf_op | source)
XLA Modules:
  0.0 21.1 jit_solution(712023609300198501)
XLA Ops:
  1.3 19.2 %fused.1 = f32[2,4,8,128]{3,2,1,0:T(8,128)S(1)} custom-call(s32[1,128]{1,0:T(1,128)} %bitcast.9, s32[1]{0:T(128)S(6)} %copy.8.count_hbm, s32[128,256]{1,0:T(8,128)} %off_hbm.1, f32[3,128,256]{2,1,0:T(8,128)} %bitcast.7, f32[3,128,256]{2,1,0:T(8,128)} %bitcast.8, f32[128,256]{1,0:T(8,128)} %weight_hbm.1), custom_call_target="tpu_custom_call" | custom-call | tf_op jit(solution)/shard_map/fused/pallas_call | solution.py:431
  20.5 0.6 %slice_bitcast_fusion = (f32[4,8,128]{2,1,0:T(8,128)}, f32[4,8,128]{2,1,0:T(8,128)}) fusion(f32[2,4,8,128]{3,2,1,0:T(8,128)S(1)} %fused.1), kind=kLoop, calls=%fused_computation | loop fusion | bytes 65536 | tf_op jit(solution)/shard_map/squeeze | solution.py:478

commit v4 on v3

--- a/solution.py
+++ b/solution.py
@@ -83,8 +83,8 @@
     tile = lax.broadcasted_iota(I32, (tiles, 1), 0)
     slot = jnp.where(tile < count, down[:, :1] * capacity + rank, -1)
     wanted = lax.broadcasted_iota(I32, (tiles, slots), 1)
-    found = jnp.where(slot == wanted, jnp.broadcast_to(tile, (tiles, slots)), -1)
-    return jnp.max(found, axis=0, keepdims=True)
+    found = jnp.where(slot == wanted, jnp.broadcast_to(tile, (tiles, slots)), tiles)
+    return jnp.min(found, axis=0, keepdims=True)
 
 
 def fused_kernel(
@@ -145,6 +145,12 @@
         pl.semaphore_signal(barrier, inc=1, device_id=friend, device_id_type=MESH)
 
     grid[...] = jnp.zeros_like(grid)
+    blank = pl.ds(tiles, SUB)
+    for half in range(halves):
+        for n in range(CHANNELS):
+            chan[half, n, blank, :] = jnp.full((SUB, LANES), 8.0 * SUB if n == CX else 0.0, F32)
+        cell_z[half, blank, :] = jnp.zeros((SUB, LANES), I32)
+
 
     for copy in loads:
         copy.wait()
@@ -169,6 +175,8 @@
 
     sub = lax.broadcasted_iota(I32, (SUB, LANES), 0)
 
+    ahead = sub + 1
+
     def layer_of(slab):
         return (sub + 4 * lax.rem(slab, 2)) & (SUB - 1)
 
@@ -182,15 +190,14 @@
         for c in range(capacity):
             lefts, rights = [], []
             entry = table[0, brick * capacity + c]
-            away = jnp.where(entry >= 0, 0.0, 8.0 * SUB)
-            tile = jnp.minimum(jnp.maximum(entry, 0), tiles - 1)
+            tile = jnp.minimum(jnp.maximum(entry, 0), tiles)
             for half in range(halves):
                 left, right = [[], [], []], [[], []]
 
                 def row(n):
                     return jnp.broadcast_to(chan[half, n, pl.ds(tile, 1), :], (SUB, LANES))
 
-                gap = layer - (row(CX) + away)
+                gap = layer - row(CX)
                 hit = [gap == float(k) for k in range(3)]
                 wx = pick(hit, [row(WX + k) for k in range(3)])
                 gx = pick(hit, [row(GX + k) for k in range(3)])
@@ -205,15 +212,16 @@
                     left[1].append(plain * wide)
                     left[2].append(third * wide)
                 z = jnp.broadcast_to(cell_z[half, pl.ds(tile, 1), :], (SUB, LANES))
-                tap = (sub - z + 1) & (SUB - 1)
+                lag = ahead - z
+                tap = lag & (SUB - 1)
                 hit = [tap == k for k in range(3)]
                 value = twice(pick(hit, [row(WZ + k) for k in range(3)]))
                 slope = twice(pick(hit, [row(GZ + k) for k in range(3)]))
-                home = ((z - 1 + tap) >> 3).astype(F32)
-                home = pair_up(home, home - 1.0)
+                home = (tap - lag).astype(F32)
+                home = pair_up(home, home - SUB)
                 zero = jnp.zeros_like(value)
                 for m in range(BZ // (2 * SUB)):
-                    here = home == jnp.bfloat16(2 * m)
+                    here = home == jnp.bfloat16(2 * SUB * m)
                     right[0].append(jnp.where(here, value, zero))
                     right[1].append(jnp.where(here, slope, zero))
                 lefts.append(jnp.concatenate(sum(left, []), axis=0))
@@ -361,13 +369,13 @@
     for step in (last - 1, last):
         for k in range(split):
             add_brick(step, k)
+        share(step, 0)
         if step < last:
             spread(step - 1, 0)
         spread(step - 1, 1)
         if step == last:
             for j in range(last - 2):
                 forward(j)
-        share(step, 0)
         for k in range(split, n_columns):
             add_brick(step, k)
         share(step, 1)
@@ -442,7 +450,7 @@
             pltpu.VMEM((1, slots), I32),
             pltpu.SMEM((1, slots), I32),
             pltpu.VMEM((tile_len // LANES, CHANNELS, tiles + SUB, LANES), F32),
-            pltpu.VMEM((tile_len // LANES, tiles, LANES), I32),
+            pltpu.VMEM((tile_len // LANES, tiles + SUB, LANES), I32),
             pltpu.VMEM((2, (n_columns * BY + 2) * SUB, BZ), F32),
             pltpu.VMEM((n_slabs, 2, 2, near, HALO_X) + block, F32),
             pltpu.VMEM((n_slabs, 2, near, HALO_X) + block, F32),

time: 21.3 us -> 20.9 us (0.981)
  Pallas kernels: 19.2 us -> 18.8 us
    pallas_call x1, Pallas kernels: 19.2 us -> 18.8 us  [fused(): pl.pallas_call(functools.partial(fused_kernel, capacity, n_slabs, n_colum...]
where the time goes in v4:
time: 20.9 us; the launch traced here: 20.7 us
  Pallas kernels  18.8 us (90%)
  between operations  1.29 us (6%)
  local copies, waits for them, and re-layouts  0.61 us (3%)
    pallas_call x1, Pallas kernels, fused(): pl.pallas_call(functools.partial(fused_kernel, capacity, n_slabs, n_colum...  18.8 us
    squeeze x1, local copies, waits for them, and re-layouts, shards(): return (both[0], both[1])  0.61 us

profile of v4, /device:TPU:0, one launch (start us, length us, event | category | flops | bytes accessed | tf_op | source)
XLA Modules:
  0.0 20.7 jit_solution(2731893434980531542)
XLA Ops:
  1.3 18.8 %fused.1 = f32[2,4,8,128]{3,2,1,0:T(8,128)S(1)} custom-call(s32[1,128]{1,0:T(1,128)} %bitcast.9, s32[1]{0:T(128)S(6)} %copy.8.count_hbm, s32[128,256]{1,0:T(8,128)} %off_hbm.1, f32[3,128,256]{2,1,0:T(8,128)} %bitcast.7, f32[3,128,256]{2,1,0:T(8,128)} %bitcast.8, f32[128,256]{1,0:T(8,128)} %weight_hbm.1), custom_call_target="tpu_custom_call" | custom-call | tf_op jit(solution)/shard_map/fused/pallas_call | solution.py:439
  20.1 0.6 %slice_bitcast_fusion = (f32[4,8,128]{2,1,0:T(8,128)}, f32[4,8,128]{2,1,0:T(8,128)}) fusion(f32[2,4,8,128]{3,2,1,0:T(8,128)S(1)} %fused.1), kind=kLoop, calls=%fused_computation | loop fusion | bytes 65536 | tf_op jit(solution)/shard_map/squeeze | solution.py:486
